TPU v7x, 32 devices: a whole 2x2x4 slice. The times are simulated.
32 devices in a mesh: res: 8 (over z, y), seq: 4 (over x, core).
Axes of the slice: x: 2, y: 2, z: 4, core: 2. Of those that a mesh axis runs over, the one named last changes fastest.
Arguments:
- alignment: bfloat16 [384, 256, 256], P('seq', 'res'), may hold values from -6 to 6
- query_weight: bfloat16 [256, 256], replicated, may hold values from -1 to 1
- w_keyval: bfloat16 [256, 512], replicated, may hold values from -0.375 to 0.375
- w_gate: bfloat16 [256, 256], replicated, may hold values from -0.375 to 0.375
- output_weight: bfloat16 [256, 256], replicated, may hold values from -0.75 to 0.75
- w_factors: bfloat16 [256, 64], replicated, may hold values from -1.5 to 1.5
- w_pair_out: bfloat16 [1024, 128], replicated, may hold values from -0.1875 to 0.1875
Outputs:
- alignment_update: bfloat16 [384, 256, 256], P('seq', 'res')
- pair_representation_update: bfloat16 [256, 256, 128], P(('res', 'seq'))
All inputs are finite; a program needn't handle non-finite values.
Results may differ from a plain program's by a relative error of at most 0.012.
The roundings to bfloat16 on the way count: a program that leaves them out, or rounds other values in their place, can miss the bound.
Values may be sent and summed in bfloat16 or wider, within the bound.
A program may use at most 256 MiB of HBM per device.

v0:
```python
import functools
import math

import jax
import jax.numpy as jnp
from jax import lax
from jax.experimental import pallas as pl
from jax.experimental.pallas import tpu as pltpu
from jax.sharding import PartitionSpec as P

HEADS = 8
HC = 32
LOG2E = 1.4426950408889634
epsilon = 1e-05
NT = (((1,), (1,)), ((), ()))


def mm(a, b):
    return jnp.dot(a, b, preferred_element_type=jnp.float32)


def mm_nt(a, b):
    return lax.dot_general(a, b, NT, preferred_element_type=jnp.float32)


MESH = pl.DeviceIdType.MESH
COUNT = 4


def attend_residues(own, everything, wq, wg, wkv, wout):
    groups, count, seqs, width = everything.shape
    hidden = HEADS * HC
    kv = mm(everything.reshape(groups * count * seqs, width), wkv).astype(jnp.bfloat16)
    kv = kv.reshape(groups, count, seqs, 2 * hidden)
    rows = own.reshape(count * seqs, width)
    queries = mm(rows, wq).astype(jnp.bfloat16)
    gating = jax.nn.sigmoid(mm(rows, wg))
    head_of = lax.broadcasted_iota(jnp.int32, (seqs, hidden), 1) // HC
    gated = []
    for n in range(count):
        q = queries[n * seqs : (n + 1) * seqs].astype(jnp.float32)
        stacked = jnp.concatenate(
            [jnp.where(head_of == h, q, 0.0).astype(jnp.bfloat16) for h in range(HEADS)], axis=0
        )
        keys = kv[:, n, :, :hidden].reshape(groups * seqs, hidden)
        values = kv[:, n, :, hidden:].reshape(groups * seqs, hidden)
        exponent = jnp.exp2(mm_nt(stacked, keys) * (LOG2E / math.sqrt(HC)))
        inverse = 1.0 / jnp.sum(exponent, axis=-1, keepdims=True)
        weighted = mm(exponent.astype(jnp.bfloat16), values)
        attended = jnp.zeros((seqs, hidden), jnp.float32)
        for h in range(HEADS):
            rows = slice(h * seqs, (h + 1) * seqs)
            attended = jnp.where(head_of == h, weighted[rows] * inverse[rows], attended)
        gated.append((gating[n * seqs : (n + 1) * seqs] * attended).astype(jnp.bfloat16))
    return mm(jnp.concatenate(gated, axis=0), wout)


def block_kernel(
    scaling,
    blocks,
    groups,
    x_ref,
    wq_ref,
    wkv_ref,
    wg_ref,
    wout_ref,
    wf_ref,
    wp_ref,
    o_ref,
    pair_ref,
    gathered,
    strided,
    pair_rows,
    spread,
    wft,
    left_all,
    right_all,
    products,
    outer,
    outgoing,
    incoming,
    cross_send,
    cross_recv,
    twin_send,
    twin_recv,
    relay_send,
    relay_recv,
    ring_send,
    ring_recv,
    share_send,
    share_recv,
    swap_send,
    swap_recv,
):
    seqs, residues, width = x_ref.shape
    depth = seqs * groups
    factor = wf_ref.shape[1] // 2
    pack = 128 // factor
    own_rows = residues // groups
    channels = pair_ref.shape[2]
    half = residues // 2
    parts = residues // COUNT
    half_parts = parts // 2
    hops = blocks // 2
    r = lax.axis_index("res")
    q = lax.axis_index("seq")
    core = lax.rem(q, 2)
    side = q // 2
    twin = q + 1 - 2 * core
    across = lax.rem(q + 2, groups)
    twin_across = lax.rem(twin + 2, groups)

    def ring_of(block):
        z, y = block // 2, lax.rem(block, 2)
        return jnp.where(y == 0, z, blocks - 1 - z)

    def block_of(place):
        return jnp.where(place < blocks // 2, 2 * place, 2 * (blocks - 1 - place) + 1)

    place = ring_of(r)
    ahead = block_of(lax.rem(place + 1, blocks))
    behind = block_of(lax.rem(place + blocks - 1, blocks))

    barrier = pltpu.get_barrier_semaphore()
    for target in ((r, twin), (r, across), (ahead, q), (behind, q)):
        pl.semaphore_signal(barrier, inc=1, device_id=target, device_id_type=MESH)
    pl.semaphore_wait(barrier, 4)

    def part_at(p):
        return lax.rem(p + side * half_parts, parts)

    def rows_of(owner, part):
        return gathered.at[owner, pl.ds(part * COUNT, COUNT)]

    def send(ref, dst, send_sem, recv_sem, target):
        return pltpu.make_async_remote_copy(
            src_ref=ref,
            dst_ref=dst,
            send_sem=send_sem,
            recv_sem=recv_sem,
            device_id=target,
            device_id_type=MESH,
        )

    def cross(owner, p, part):
        block = rows_of(owner, part)
        return send(block, block, cross_send.at[p], cross_recv.at[p], (r, across))

    def direct(owner, p, part):
        block = rows_of(owner, part)
        return send(block, block, twin_send.at[p], twin_recv.at[p], (r, twin))

    def relay(owner, p, part):
        block = rows_of(owner, part)
        return send(block, block, relay_send.at[p], relay_recv.at[p], (r, twin))

    step = 8
    for turn in range(2):
        which = (1 - side) if turn == 0 else side
        base = pl.multiple_of(which * half, half)

        def norm(i, carry):
            values = (
                x_ref[pl.ds(i * step, step), pl.ds(base, half), :]
                .reshape(step * half, width)
                .astype(jnp.float32)
            )
            centered = values - jnp.mean(values, axis=-1, keepdims=True)
            spread = jnp.mean(centered * centered, axis=-1, keepdims=True)
            normed = centered * lax.rsqrt(spread + epsilon)
            for part in range(width // 128):
                strided[part, pl.ds(i * (step * half), step * half), :] = normed[
                    :, part * 128 : (part + 1) * 128
                ]
            return carry

        lax.fori_loop(0, seqs // step, norm, 0)

        def move(k, carry):
            for n in range(COUNT):
                for part in range(width // 128):
                    gathered[q, base + k * COUNT + n, :, part * 128 : (part + 1) * 128] = strided[
                        part, pl.ds(k * COUNT + n, seqs, half), :
                    ].astype(jnp.bfloat16)
            return carry

        def start_across(k, carry):
            cross(q, turn * half_parts + k, which * half_parts + k).start()
            return carry

        def move_and_start(k, carry):
            move(k, carry)
            return start_across(k, carry)

        lax.fori_loop(0, half_parts, move_and_start, 0)

    def start_twin(p, carry):
        direct(q, p, part_at(p)).start()
        return carry

    lax.fori_loop(0, parts, start_twin, 0)

    both_factors = 2 * factor
    unit = jnp.where(
        lax.broadcasted_iota(jnp.int32, (both_factors, both_factors), 0)
        == lax.broadcasted_iota(jnp.int32, (both_factors, both_factors), 1),
        1.0,
        0.0,
    ).astype(jnp.bfloat16)
    wft[...] = mm_nt(unit, wf_ref[...]).astype(jnp.bfloat16)
    pair_rows[...] = wp_ref[...].astype(jnp.float32)
    spread[...] = jnp.zeros_like(spread)
    for e in range(factor):
        rows = pair_rows[pl.ds(e, factor, factor), :].astype(jnp.bfloat16)
        for k in range(pack):
            start = (e * pack + k) * factor
            spread[start : start + factor, k * channels : (k + 1) * channels] = rows

    share = COUNT // 2

    def mine(sub):
        return pl.ds(sub * COUNT + core * share, share)

    def twins(sub):
        return pl.ds(sub * COUNT + (1 - core) * share, share)

    def ring_copy(way, sub, hop):
        shift = blocks - hop if way == 0 else hop
        block = block_of(lax.rem(place + shift, blocks))
        ref = right_all.at[block, mine(sub)]
        return send(
            ref,
            ref,
            ring_send.at[way, sub, hop],
            ring_recv.at[way, sub, hop],
            ((ahead if way == 0 else behind), q),
        )

    def landed(way, hop):
        shift = blocks - hop - 1 if way == 0 else hop + 1
        return block_of(lax.rem(place + shift, blocks))

    def arrive(way, sub, hop):
        ref = right_all.at[landed(way, hop), mine(sub)]
        send(
            ref,
            ref,
            ring_send.at[way, sub, hop],
            ring_recv.at[way, sub, hop],
            ((ahead if way == 0 else behind), q),
        ).wait_recv()

    def share_copy(way, sub, hop, outward=True):
        ref = right_all.at[landed(way, hop), mine(sub) if outward else twins(sub)]
        return send(
            ref, ref, share_send.at[way, sub, hop], share_recv.at[way, sub, hop], (r, twin)
        )

    ways = (hops, blocks - 1 - hops)

    def advance(sub, hop):
        for way in range(2):

            @pl.when((hop > 0) & (hop <= ways[way]))
            def _():
                arrive(way, sub, hop - 1)

            @pl.when((hop >= 0) & (hop < ways[way]))
            def _():
                ring_copy(way, sub, hop).start()

            @pl.when((hop > 0) & (hop <= ways[way]))
            def _():
                share_copy(way, sub, hop - 1).start()

    def advance_all(p):
        for sub in range(half_parts):
            advance(sub, p - sub)

    def take_across(p):
        cross(across, p, part_at(p)).wait_recv()
        relay(across, p, part_at(p)).start()

    take_across(0)

    def one_part(p, carry):
        part = part_at(p)
        direct(twin, p, part).wait_recv()
        relay(twin_across, p, part).wait_recv()
        everything = gathered[:, pl.ds(part * COUNT, COUNT)]
        for n in range(COUNT):
            both = mm_nt(wft[...], everything[:, n].reshape(depth, width)).astype(jnp.bfloat16)
            left_all[part * COUNT + n] = both[:factor]

            @pl.when(p < half_parts)
            def _():
                right_all[r, p * COUNT + n] = both[factor:]

        few = COUNT // 2
        for turn in range(2):
            first = part * COUNT + turn * few
            update = attend_residues(
                gathered[q, pl.ds(first, few)],
                gathered[:, pl.ds(first, few)],
                wq_ref[...],
                wg_ref[...],
                wkv_ref[...],
                wout_ref[...],
            )
            for n in range(few):
                for piece in range(width // 128):
                    strided[piece, pl.ds(first + n, seqs, residues), :] = update[
                        n * seqs : (n + 1) * seqs, piece * 128 : (piece + 1) * 128
                    ]
            if turn == 0:

                @pl.when(p + 1 < parts)
                def _():
                    take_across(p + 1)

        advance_all(p)
        return carry

    lax.fori_loop(0, parts, one_part, 0)

    def late(p, carry):
        advance_all(p)
        return carry

    lax.fori_loop(parts, half_parts + hops, late, 0)

    for way in range(2):
        for sub in range(half_parts):

            def shared(hop, carry):
                share_copy(way, sub, hop, False).wait_recv()
                return carry

            lax.fori_loop(0, ways[way], shared, 0)

    lanes = own_rows * factor
    span = blocks * half

    def pair_of(owner):
        left = left_all[pl.ds(owner * own_rows, own_rows)].reshape(lanes, depth)

        def one_block(b, inner):
            value = mm_nt(right_all[b].reshape(half * factor, depth), left) * scaling
            for g in range(lanes // 128):
                products[g] = value[:, g * 128 : (g + 1) * 128]
            for e in range(factor):
                for g in range(lanes // 128):
                    outer[
                        pl.ds(pl.multiple_of(g * span + b * half, half), half),
                        e * 128 : (e + 1) * 128,
                    ] = products[g, pl.ds(e, half, factor), :].astype(jnp.bfloat16)
            return inner

        lax.fori_loop(0, blocks, one_block, 0)
        return mm(outer[...], spread[...]).astype(jnp.bfloat16)

    def cut(pair, i):
        g, k = i // pack, i % pack
        return pair[g * span : (g + 1) * span, k * channels : (k + 1) * channels]

    def swap_copy():
        return send(outgoing, incoming, swap_send, swap_recv, (r, across))

    pair = pair_of(across)
    for i in range(own_rows):
        outgoing[i] = cut(pair, i)
    swap_copy().start()

    def place_rows(i, which, value):
        for b in range(blocks):
            start = pl.multiple_of(b * residues + which * half, half)
            pair_ref[i, pl.ds(start, half), :] = value[b * half : (b + 1) * half]

    pair = pair_of(q)
    for i in range(own_rows):
        place_rows(i, side, cut(pair, i))

    def finish(i, carry):
        for piece in range(width // 128):
            o_ref[pl.ds(i * step, step), :, piece * 128 : (piece + 1) * 128] = (
                strided[piece, pl.ds(i * (step * residues), step * residues), :]
                .astype(jnp.bfloat16)
                .reshape(step, residues, 128)
            )
        return carry

    lax.fori_loop(0, seqs // step, finish, 0)
    swap_copy().wait_recv()
    for i in range(own_rows):
        place_rows(i, 1 - side, incoming[i])

    def drain(p, carry):
        cross(q, p, lax.rem(part_at(p) + half_parts, parts)).wait_send()
        direct(q, p, part_at(p)).wait_send()
        relay(across, p, part_at(p)).wait_send()
        return carry

    lax.fori_loop(0, parts, drain, 0)
    for way in range(2):
        for sub in range(half_parts):

            def drain_ring(hop, carry):
                ring_copy(way, sub, hop).wait_send()
                share_copy(way, sub, hop).wait_send()
                return carry

            lax.fori_loop(0, ways[way], drain_ring, 0)
    swap_copy().wait_send()


def per_device(alignment, query_weight, w_keyval, w_gate, output_weight, w_factors, w_pair_out):
    seqs, residues, width = alignment.shape
    groups = lax.axis_size("seq")
    blocks = lax.axis_size("res")
    depth = seqs * groups
    factor = w_factors.shape[1] // 2
    channels = w_pair_out.shape[1]
    own_rows = residues // groups
    half = residues // 2
    parts = residues // COUNT
    hops = blocks // 2
    pack = 128 // factor
    subs = parts // 2
    span = blocks * half
    vmem = pl.BlockSpec(memory_space=pltpu.VMEM)
    dma = pltpu.SemaphoreType.DMA
    return pl.pallas_call(
        functools.partial(block_kernel, 1.0 / depth, blocks, groups),
        in_specs=[vmem] * 7,
        out_specs=[vmem] * 2,
        out_shape=[
            jax.ShapeDtypeStruct((seqs, residues, width), jnp.bfloat16),
            jax.ShapeDtypeStruct((own_rows, blocks * residues, channels), jnp.bfloat16),
        ],
        scratch_shapes=[
            pltpu.VMEM((groups, residues, seqs, width), jnp.bfloat16),
            pltpu.VMEM((width // 128, seqs * residues, 128), jnp.float32),
            pltpu.VMEM((factor * factor, channels), jnp.float32),
            pltpu.VMEM((factor * 128, pack * channels), jnp.bfloat16),
            pltpu.VMEM((2 * factor, width), jnp.bfloat16),
            pltpu.VMEM((residues, factor, depth), jnp.bfloat16),
            pltpu.VMEM((blocks, half, factor, depth), jnp.bfloat16),
            pltpu.VMEM((own_rows // pack, half * factor, 128), jnp.float32),
            pltpu.VMEM((own_rows // pack * span, factor * 128), jnp.bfloat16),
            pltpu.VMEM((own_rows, span, channels), jnp.bfloat16),
            pltpu.VMEM((own_rows, span, channels), jnp.bfloat16),
            dma((parts,)),
            dma((parts,)),
            dma((parts,)),
            dma((parts,)),
            dma((parts,)),
            dma((parts,)),
            dma((2, subs, hops)),
            dma((2, subs, hops)),
            dma((2, subs, hops)),
            dma((2, subs, hops)),
            dma,
            dma,
        ],
        compiler_params=pltpu.CompilerParams(
            vmem_limit_bytes=62 * 1024 * 1024, collective_id=0, has_side_effects=True
        ),
        name="block",
    )(alignment, query_weight, w_keyval, w_gate, output_weight, w_factors, w_pair_out)


def solution(mesh):
    in_specs = (P("seq", "res", None), P(), P(), P(), P(), P(), P())
    out_specs = (P("seq", "res", None), P(("res", "seq"), None, None))
    return jax.shard_map(
        per_device, mesh=mesh, in_specs=in_specs, out_specs=out_specs, check_vma=False
    )
```

profile of v0, /device:TPU:0, one launch (start us, length us, event | category | flops | bytes accessed | tf_op | source)
XLA Modules:
  0.0 77.6 jit_solution(11326713306048195281)
XLA Ops:
  0.6 1.5 %copy.9.wf_ref = bf16[256,64]{1,0:T(8,128)(2,1)} copy(bf16[256,64]{0,1:T(8,128)(2,1)} %param.12) | data formatting | bytes 65536 | tf_op args[5]
  2.1 72.0 %block.1 = (bf16[96,32,256]{2,1,0:T(8,128)(2,1)}, bf16[8,256,128]{2,1,0:T(8,128)(2,1)}) custom-call(bf16[96,32,256]{2,1,0:T(8,128)(2,1)} %x_ref.1, bf16[256,256]{1,0:T(8,128)(2,1)} %wq_ref.1, bf16[256,512]{1,0:T(8,128)(2,1)} %wkv_ref.1, bf16[256,256]{1,0:T(8,128)(2,1)} %wg_ref.1, bf16[256,256]{1,0:T(8,128)(2,1)} %wout_ref.1, bf16[256,64]{1,0:T(8,128)(2,1)} %copy.9.wf_ref, ...), custom_call_target="tpu_custom_call" | custom-call | tf_op jit(solution)/shard_map/block/pallas_call | solution.py:432
  74.1 0.0 copy-start
  74.1 2.7 %copy.12 = bf16[96,32,256]{2,1,0:T(8,128)(2,1)} copy(bf16[96,32,256]{2,1,0:T(8,128)(2,1)} %get-tuple-element.4) | data formatting | bytes 3145728
  76.8 0.0 copy-done
  76.8 0.8 %copy.13 = bf16[8,256,128]{2,1,0:T(8,128)(2,1)} copy(bf16[8,256,128]{2,1,0:T(8,128)(2,1)S(1)} %copy-done) | data formatting | bytes 1048576
Async XLA Ops:
  74.1 2.7 %copy-start = (bf16[8,256,128]{2,1,0:T(8,128)(2,1)S(1)}, bf16[8,256,128]{2,1,0:T(8,128)(2,1)}, u32[]{:S(2)}) copy-start(bf16[8,256,128]{2,1,0:T(8,128)(2,1)} %get-tuple-element.5) | copy-start | bytes 1572868
where the time goes:
time: 78 us; the launch traced here: 77.6 us
  Pallas kernels  72 us (92%)
  local copies, waits for them, and re-layouts  5.02 us (6%)
    pallas_call x1, Pallas kernels, per_device(): pl.pallas_call(functools.partial(block_kernel, 1.0 / depth, blocks, group...  72 us
    unnamed x5, local copies, waits for them, and re-layouts  5.02 us

commit v1 on v0

--- a/solution.py
+++ b/solution.py
@@ -24,35 +24,60 @@
 
 
 MESH = pl.DeviceIdType.MESH
-COUNT = 4
-
-
-def attend_residues(own, everything, wq, wg, wkv, wout):
-    groups, count, seqs, width = everything.shape
+COUNT = 2
+WIDE = 256
+
+
+SCALE = LOG2E / math.sqrt(HC)
+
+
+def chunk_heads(chunk, seqs, wide):
+    first = chunk * wide // seqs
+    last = ((chunk + 1) * wide - 1) // seqs + 1
+    return first, min(last, HEADS)
+
+
+def prepare_keys(everything, wkv, keys):
     hidden = HEADS * HC
-    kv = mm(everything.reshape(groups * count * seqs, width), wkv).astype(jnp.bfloat16)
-    kv = kv.reshape(groups, count, seqs, 2 * hidden)
-    rows = own.reshape(count * seqs, width)
-    queries = mm(rows, wq).astype(jnp.bfloat16)
-    gating = jax.nn.sigmoid(mm(rows, wg))
+    keys[...] = mm(everything, wkv[:, :hidden]).astype(jnp.bfloat16)
+
+
+def prepare_values(everything, wkv, values):
+    hidden = HEADS * HC
+    values[...] = lax.dot_general(
+        wkv[:, hidden:], everything, (((0,), (1,)), ((), ())), preferred_element_type=jnp.float32
+    ).astype(jnp.bfloat16)
+
+
+def prepare_queries(own, wq, wg, stacked, gates):
+    seqs = own.shape[0]
+    hidden = HEADS * HC
+    q = mm(own, wq[...]).astype(jnp.bfloat16).astype(jnp.float32)
     head_of = lax.broadcasted_iota(jnp.int32, (seqs, hidden), 1) // HC
-    gated = []
-    for n in range(count):
-        q = queries[n * seqs : (n + 1) * seqs].astype(jnp.float32)
-        stacked = jnp.concatenate(
-            [jnp.where(head_of == h, q, 0.0).astype(jnp.bfloat16) for h in range(HEADS)], axis=0
-        )
-        keys = kv[:, n, :, :hidden].reshape(groups * seqs, hidden)
-        values = kv[:, n, :, hidden:].reshape(groups * seqs, hidden)
-        exponent = jnp.exp2(mm_nt(stacked, keys) * (LOG2E / math.sqrt(HC)))
-        inverse = 1.0 / jnp.sum(exponent, axis=-1, keepdims=True)
-        weighted = mm(exponent.astype(jnp.bfloat16), values)
-        attended = jnp.zeros((seqs, hidden), jnp.float32)
-        for h in range(HEADS):
-            rows = slice(h * seqs, (h + 1) * seqs)
-            attended = jnp.where(head_of == h, weighted[rows] * inverse[rows], attended)
-        gated.append((gating[n * seqs : (n + 1) * seqs] * attended).astype(jnp.bfloat16))
-    return mm(jnp.concatenate(gated, axis=0), wout)
+    for h in range(HEADS):
+        stacked[h * seqs : (h + 1) * seqs, :] = jnp.where(head_of == h, q, 0.0).astype(jnp.bfloat16)
+    gates[...] = jax.nn.sigmoid(mm(own, wg[...]))
+
+
+def score(keys, stacked, chunk, wide):
+    rows = stacked[chunk * wide : (chunk + 1) * wide]
+    exponent = jnp.exp2(mm_nt(keys[...], rows) * SCALE)
+    return exponent.astype(jnp.bfloat16), 1.0 / jnp.sum(exponent, axis=0, keepdims=True)
+
+
+def weigh(values, attended, chunk, wide, seqs, weights, inverse):
+    first, last = chunk_heads(chunk, seqs, wide)
+    mixed = mm(values[first * HC : last * HC], weights) * inverse
+    for h in range(first, last):
+        low, high = max(h * seqs, chunk * wide), min((h + 1) * seqs, (chunk + 1) * wide)
+        attended[h * HC : (h + 1) * HC, low - h * seqs : high - h * seqs] = mixed[
+            (h - first) * HC : (h - first + 1) * HC, low - chunk * wide : high - chunk * wide
+        ]
+
+
+def finish_residue(attended, gates, wout):
+    seqs = gates.shape[0]
+    return mm((gates[...] * attended[...].T[:seqs]).astype(jnp.bfloat16), wout[...])
 
 
 def block_kernel(
@@ -72,7 +97,6 @@
     strided,
     pair_rows,
     spread,
-    wft,
     left_all,
     right_all,
     products,
@@ -91,10 +115,11 @@
     share_recv,
     swap_send,
     swap_recv,
+    *stages,
 ):
     seqs, residues, width = x_ref.shape
     depth = seqs * groups
-    factor = wf_ref.shape[1] // 2
+    factor = wf_ref.shape[0] // 2
     pack = 128 // factor
     own_rows = residues // groups
     channels = pair_ref.shape[2]
@@ -200,14 +225,6 @@
 
     lax.fori_loop(0, parts, start_twin, 0)
 
-    both_factors = 2 * factor
-    unit = jnp.where(
-        lax.broadcasted_iota(jnp.int32, (both_factors, both_factors), 0)
-        == lax.broadcasted_iota(jnp.int32, (both_factors, both_factors), 1),
-        1.0,
-        0.0,
-    ).astype(jnp.bfloat16)
-    wft[...] = mm_nt(unit, wf_ref[...]).astype(jnp.bfloat16)
     pair_rows[...] = wp_ref[...].astype(jnp.float32)
     spread[...] = jnp.zeros_like(spread)
     for e in range(factor):
@@ -283,36 +300,61 @@
 
     take_across(0)
 
+    slots = (stages[: len(stages) // 2], stages[len(stages) // 2 :])
+    chunks = HEADS * seqs // WIDE
+
+    def residue_at(p, n):
+        return part_at(lax.rem(p + parts + n // COUNT, parts)) * COUNT + n % COUNT
+
+    def weigh_last(slot):
+        weigh(
+            slot[1], slot[4], chunks - 1, WIDE, seqs, slot[5][...], slot[6][0:1, :]
+        )
+
+    def emit(slot, residue):
+        update = finish_residue(slot[4], slot[3], wout_ref)
+        for piece in range(width // 128):
+            strided[piece, pl.ds(residue, seqs, residues), :] = update[
+                :, piece * 128 : (piece + 1) * 128
+            ]
+
+    def attend(slot, other, fresh, emitted):
+        everything = gathered[:, fresh].reshape(depth, width) if fresh is not None else None
+        held = [score(slot[0], slot[2], 0, WIDE)]
+        weigh_last(other)
+        for c in range(1, chunks):
+            now = score(slot[0], slot[2], c, WIDE)
+            if c == chunks - 1:
+                slot[5][...], slot[6][0:1, :] = now
+            if c == 1:
+                emit(other, emitted)
+                if fresh is not None:
+                    prepare_queries(gathered[q, fresh], wq_ref, wg_ref, other[2], other[3])
+            held.append(now)
+            weigh(slot[1], slot[4], c - 1, WIDE, seqs, *held[c - 1])
+            if c == 1 and fresh is not None:
+                prepare_keys(everything, wkv_ref, other[0])
+        if fresh is not None:
+            prepare_values(everything, wkv_ref, other[1])
+
     def one_part(p, carry):
         part = part_at(p)
         direct(twin, p, part).wait_recv()
         relay(twin_across, p, part).wait_recv()
         everything = gathered[:, pl.ds(part * COUNT, COUNT)]
         for n in range(COUNT):
-            both = mm_nt(wft[...], everything[:, n].reshape(depth, width)).astype(jnp.bfloat16)
+            both = mm_nt(wf_ref[...], everything[:, n].reshape(depth, width)).astype(jnp.bfloat16)
             left_all[part * COUNT + n] = both[:factor]
 
             @pl.when(p < half_parts)
             def _():
                 right_all[r, p * COUNT + n] = both[factor:]
 
-        few = COUNT // 2
-        for turn in range(2):
-            first = part * COUNT + turn * few
-            update = attend_residues(
-                gathered[q, pl.ds(first, few)],
-                gathered[:, pl.ds(first, few)],
-                wq_ref[...],
-                wg_ref[...],
-                wkv_ref[...],
-                wout_ref[...],
+        for n in range(COUNT):
+            attend(
+                slots[(n + 1) % 2], slots[n % 2], residue_at(p, n), residue_at(p, n - 2)
             )
-            for n in range(few):
-                for piece in range(width // 128):
-                    strided[piece, pl.ds(first + n, seqs, residues), :] = update[
-                        n * seqs : (n + 1) * seqs, piece * 128 : (piece + 1) * 128
-                    ]
-            if turn == 0:
+            if n == 0:
 
                 @pl.when(p + 1 < parts)
                 def _():
@@ -322,6 +364,9 @@
         return carry
 
     lax.fori_loop(0, parts, one_part, 0)
+    attend(slots[1], slots[0], None, residue_at(parts - 1, COUNT - 2))
+    weigh_last(slots[1])
+    emit(slots[1], residue_at(parts - 1, COUNT - 1))
 
     def late(p, carry):
         advance_all(p)
@@ -419,6 +464,16 @@
     blocks = lax.axis_size("res")
     depth = seqs * groups
     factor = w_factors.shape[1] // 2
+    hidden = HEADS * HC
+    stage = [
+        pltpu.VMEM((depth, hidden), jnp.bfloat16),
+        pltpu.VMEM((hidden, depth), jnp.bfloat16),
+        pltpu.VMEM((HEADS * seqs, hidden), jnp.bfloat16),
+        pltpu.VMEM((seqs, hidden), jnp.float32),
+        pltpu.VMEM((hidden, 128), jnp.float32),
+        pltpu.VMEM((depth, WIDE), jnp.bfloat16),
+        pltpu.VMEM((8, WIDE), jnp.float32),
+    ]
     channels = w_pair_out.shape[1]
     own_rows = residues // groups
     half = residues // 2
@@ -442,7 +497,6 @@
             pltpu.VMEM((width // 128, seqs * residues, 128), jnp.float32),
             pltpu.VMEM((factor * factor, channels), jnp.float32),
             pltpu.VMEM((factor * 128, pack * channels), jnp.bfloat16),
-            pltpu.VMEM((2 * factor, width), jnp.bfloat16),
             pltpu.VMEM((residues, factor, depth), jnp.bfloat16),
             pltpu.VMEM((blocks, half, factor, depth), jnp.bfloat16),
             pltpu.VMEM((own_rows // pack, half * factor, 128), jnp.float32),
@@ -461,12 +515,13 @@
             dma((2, subs, hops)),
             dma,
             dma,
-        ],
+        ]
+        + stage * 2,
         compiler_params=pltpu.CompilerParams(
             vmem_limit_bytes=62 * 1024 * 1024, collective_id=0, has_side_effects=True
         ),
         name="block",
-    )(alignment, query_weight, w_keyval, w_gate, output_weight, w_factors, w_pair_out)
+    )(alignment, query_weight, w_keyval, w_gate, output_weight, w_factors.T, w_pair_out)
 
 
 def solution(mesh):

time: 78 us -> 85.3 us (1.094)
  Pallas kernels: 72 us -> 81 us
  local copies, waits for them, and re-layouts: 5.02 us -> 3.52 us
    pallas_call x1, Pallas kernels: 72 us -> 81 us  [per_device(): pl.pallas_call(functools.partial(block_kernel, 1.0 / depth, blocks, group...]
    unnamed x5 -> x4, local copies, waits for them, and re-layouts: 5.02 us -> 3.52 us
where the time goes in v1:
time: 85.3 us; the launch traced here: 85.2 us
  Pallas kernels  81 us (95%)
  local copies, waits for them, and re-layouts  3.52 us (4%)
    pallas_call x1, Pallas kernels, per_device(): pl.pallas_call(functools.partial(block_kernel, 1.0 / depth, blocks, group...  81 us
    unnamed x4, local copies, waits for them, and re-layouts  3.52 us

profile of v1, /device:TPU:0, one launch (start us, length us, event | category | flops | bytes accessed | tf_op | source)
XLA Modules:
  0.0 85.2 jit_solution(11709635530372578419)
XLA Ops:
  0.6 81.0 %block.1 = (bf16[96,32,256]{2,1,0:T(8,128)(2,1)}, bf16[8,256,128]{2,1,0:T(8,128)(2,1)}) custom-call(bf16[96,32,256]{2,1,0:T(8,128)(2,1)} %x_ref.1, bf16[256,256]{1,0:T(8,128)(2,1)} %wq_ref.1, bf16[256,512]{1,0:T(8,128)(2,1)} %wkv_ref.1, bf16[256,256]{1,0:T(8,128)(2,1)} %wg_ref.1, bf16[256,256]{1,0:T(8,128)(2,1)} %wout_ref.1, bf16[64,256]{1,0:T(8,128)(2,1)} %bitcast.1, ...), custom_call_target="tpu_custom_call" | custom-call | tf_op jit(solution)/shard_map/block/pallas_call | solution.py:487
  81.6 0.0 copy-start
  81.6 2.7 %copy.11 = bf16[96,32,256]{2,1,0:T(8,128)(2,1)} copy(bf16[96,32,256]{2,1,0:T(8,128)(2,1)} %get-tuple-element.4) | data formatting | bytes 3145728
  84.4 0.0 copy-done
  84.4 0.8 copy.12
Async XLA Ops:
  81.6 2.7 %copy-start = (bf16[8,256,128]{2,1,0:T(8,128)(2,1)S(1)}, bf16[8,256,128]{2,1,0:T(8,128)(2,1)}, u32[]{:S(2)}) copy-start(bf16[8,256,128]{2,1,0:T(8,128)(2,1)} %get-tuple-element.5) | copy-start | bytes 1572868

commit v2 on v1

v2 whole, which is shorter than its diff:
```python
import functools
import math

import jax
import jax.numpy as jnp
from jax import lax
from jax.experimental import pallas as pl
from jax.experimental.pallas import tpu as pltpu
from jax.sharding import PartitionSpec as P

HEADS = 8
HC = 32
LOG2E = 1.4426950408889634
epsilon = 1e-05
NT = (((1,), (1,)), ((), ()))


def mm(a, b):
    return jnp.dot(a, b, preferred_element_type=jnp.float32)


def mm_nt(a, b):
    return lax.dot_general(a, b, NT, preferred_element_type=jnp.float32)


MESH = pl.DeviceIdType.MESH
COUNT = 2
WIDE = 256
PITCH_PAD = 4
FIRST_EVENT = 3
EARLY_PARTS = 2


SCALE = LOG2E / math.sqrt(HC)


def chunk_heads(chunk, seqs, wide):
    first = chunk * wide // seqs
    last = ((chunk + 1) * wide - 1) // seqs + 1
    return first, min(last, HEADS)


def prepare_keys(everything, wkv, keys):
    hidden = HEADS * HC
    keys[...] = mm(everything, wkv[:, :hidden]).astype(jnp.bfloat16)


def prepare_values(everything, wkv, values):
    hidden = HEADS * HC
    values[...] = lax.dot_general(
        wkv[:, hidden:], everything, (((0,), (1,)), ((), ())), preferred_element_type=jnp.float32
    ).astype(jnp.bfloat16)


def prepare_queries(own, wq, wg, stacked, gates):
    seqs = own.shape[0]
    hidden = HEADS * HC
    q = mm(own, wq[...]).astype(jnp.bfloat16).astype(jnp.float32)
    head_of = lax.broadcasted_iota(jnp.int32, (seqs, hidden), 1) // HC
    for h in range(HEADS):
        stacked[h * seqs : (h + 1) * seqs, :] = jnp.where(head_of == h, q, 0.0).astype(jnp.bfloat16)
    gates[...] = jax.nn.sigmoid(mm(own, wg[...]))


def score(keys, stacked, chunk, wide):
    rows = stacked[chunk * wide : (chunk + 1) * wide]
    exponent = jnp.exp2(mm_nt(keys[...], rows) * SCALE)
    return exponent.astype(jnp.bfloat16), 1.0 / jnp.sum(exponent, axis=0, keepdims=True)


def weigh(values, attended, chunk, wide, seqs, weights, inverse):
    first, last = chunk_heads(chunk, seqs, wide)
    mixed = mm(values[first * HC : last * HC], weights) * inverse
    for h in range(first, last):
        low, high = max(h * seqs, chunk * wide), min((h + 1) * seqs, (chunk + 1) * wide)
        attended[h * HC : (h + 1) * HC, low - h * seqs : high - h * seqs] = mixed[
            (h - first) * HC : (h - first + 1) * HC, low - chunk * wide : high - chunk * wide
        ]


def finish_residue(attended, gates, wout):
    seqs = gates.shape[0]
    return mm((gates[...] * attended[...].T[:seqs]).astype(jnp.bfloat16), wout[...])


def block_kernel(
    scaling,
    blocks,
    groups,
    x_ref,
    wq_ref,
    wkv_ref,
    wg_ref,
    wout_ref,
    wf_ref,
    wp_ref,
    o_ref,
    pair_ref,
    gathered,
    strided,
    pair_rows,
    spread,
    placed,
    left_rows,
    left_all,
    right_all,
    outer,
    products,
    cross_send,
    cross_recv,
    twin_send,
    twin_recv,
    relay_send,
    relay_recv,
    factor_send,
    factor_recv,
    ring_send,
    ring_recv,
    share_send,
    share_recv,
    *stages,
):
    seqs, residues, width = x_ref.shape
    depth = seqs * groups
    factor = wf_ref.shape[0] // 2
    pack = 128 // factor
    own_rows = residues // groups
    channels = pair_ref.shape[2]
    half = residues // 2
    parts = residues // COUNT
    half_parts = parts // 2
    hops = blocks // 2
    pitch = residues + PITCH_PAD
    r = lax.axis_index("res")
    q = lax.axis_index("seq")
    core = lax.rem(q, 2)
    side = q // 2
    twin = q + 1 - 2 * core
    across = lax.rem(q + 2, groups)
    twin_across = lax.rem(twin + 2, groups)

    def ring_of(block):
        z, y = block // 2, lax.rem(block, 2)
        return jnp.where(y == 0, z, blocks - 1 - z)

    def block_of(place):
        return jnp.where(place < blocks // 2, 2 * place, 2 * (blocks - 1 - place) + 1)

    place = ring_of(r)
    ahead = block_of(lax.rem(place + 1, blocks))
    behind = block_of(lax.rem(place + blocks - 1, blocks))

    barrier = pltpu.get_barrier_semaphore()
    for target in ((r, twin), (r, across), (ahead, q), (behind, q)):
        pl.semaphore_signal(barrier, inc=1, device_id=target, device_id_type=MESH)
    pl.semaphore_wait(barrier, 4)

    def part_at(p):
        return lax.rem(p + side * half_parts, parts)

    def rows_of(owner, part):
        return gathered.at[owner, pl.ds(part * COUNT, COUNT)]

    def send(ref, send_sem, recv_sem, target):
        return pltpu.make_async_remote_copy(
            src_ref=ref,
            dst_ref=ref,
            send_sem=send_sem,
            recv_sem=recv_sem,
            device_id=target,
            device_id_type=MESH,
        )

    def cross(owner, p, part):
        return send(rows_of(owner, part), cross_send.at[p], cross_recv.at[p], (r, across))

    def direct(owner, p, part):
        return send(rows_of(owner, part), twin_send.at[p], twin_recv.at[p], (r, twin))

    def relay(owner, p, part):
        return send(rows_of(owner, part), relay_send.at[p], relay_recv.at[p], (r, twin))

    def cross_own(p):
        return cross(q, p, lax.rem(part_at(p) + half_parts, parts))

    step = 8
    for turn in range(2):
        which = (1 - side) if turn == 0 else side
        base = pl.multiple_of(which * half, half)

        def norm(i, carry):
            values = (
                x_ref[pl.ds(i * step, step), pl.ds(base, half), :]
                .reshape(step * half, width)
                .astype(jnp.float32)
            )
            centered = values - jnp.mean(values, axis=-1, keepdims=True)
            variance = jnp.mean(centered * centered, axis=-1, keepdims=True)
            normed = centered * lax.rsqrt(variance + epsilon)
            for part in range(width // 128):
                for k in range(step):
                    strided[part, pl.ds((i * step + k) * pitch, half), :] = normed[
                        k * half : (k + 1) * half, part * 128 : (part + 1) * 128
                    ]
            return carry

        lax.fori_loop(0, seqs // step, norm, 0, unroll=2)

        def move(k, carry):
            for n in range(COUNT):
                for part in range(width // 128):
                    gathered[q, base + k * COUNT + n, :, part * 128 : (part + 1) * 128] = strided[
                        part, pl.ds(k * COUNT + n, seqs, pitch), :
                    ].astype(jnp.bfloat16)
            return carry

        if turn == 0:
            for k in range(EARLY_PARTS):
                move(k, 0)
                cross_own(k).start()
            lax.fori_loop(EARLY_PARTS, half_parts, move, 0, unroll=2)
        else:
            lax.fori_loop(0, half_parts, move, 0, unroll=2)

    def start_twin(p, carry):
        direct(q, p, part_at(p)).start()
        return carry

    lax.fori_loop(0, parts, start_twin, 0)

    row = lax.broadcasted_iota(jnp.int32, (factor, pack * 128), 0)
    lane = lax.broadcasted_iota(jnp.int32, (factor, pack * 128), 1)
    chosen = jnp.where(lax.rem(lane, 128) == (lane // 128) * factor + row, 1.0, 0.0)
    placed[...] = lax.dot_general(
        wf_ref[factor:],
        chosen.astype(jnp.bfloat16),
        (((0,), (0,)), ((), ())),
        preferred_element_type=jnp.float32,
    ).astype(jnp.bfloat16)

    for g in range(residues // pack):
        total = mm(gathered[q, g * pack], placed[:, :128])
        for k in range(1, pack):
            total = total + mm(gathered[q, g * pack + k], placed[:, k * 128 : (k + 1) * 128])
        right_all[r, q, :, g * 128 : (g + 1) * 128] = total.astype(jnp.bfloat16)

    def factor_copy(kind, owner):
        target = (r, across) if kind == 0 else (r, twin)
        return send(right_all.at[r, owner], factor_send.at[kind], factor_recv.at[kind], target)

    def owner_of(piece, own=True):
        if own:
            return jnp.where(piece == 0, q, across)
        return jnp.where(piece == 0, twin, twin_across)

    def shifted(way, hop):
        return block_of(lax.rem(place + (blocks - hop if way == 0 else hop), blocks))

    def neighbour(way):
        return ((ahead if way == 0 else behind), q)

    def ring_copy(way, piece, hop):
        ref = right_all.at[shifted(way, hop), owner_of(piece)]
        sems = (ring_send.at[way, piece, hop], ring_recv.at[way, piece, hop])
        return send(ref, *sems, neighbour(way))

    def arrival(way, piece, hop):
        ref = right_all.at[shifted(way, hop + 1), owner_of(piece)]
        sems = (ring_send.at[way, piece, hop], ring_recv.at[way, piece, hop])
        return send(ref, *sems, neighbour(way))

    def share_copy(way, piece, hop, outward=True):
        ref = right_all.at[shifted(way, hop + 1), owner_of(piece, outward)]
        sems = (share_send.at[way, piece, hop], share_recv.at[way, piece, hop])
        return send(ref, *sems, (r, twin))

    def reach(way, piece):
        return jnp.where(piece == way, hops, hops - 1)

    def event(piece, hop):
        for way in range(2):

            @pl.when(hop < reach(way, piece))
            def _():
                arrival(way, piece, hop).wait_recv()

            @pl.when(hop + 1 < reach(way, piece))
            def _():
                ring_copy(way, piece, hop + 1).start()

            @pl.when(hop < reach(way, piece))
            def _():
                share_copy(way, piece, hop).start()

    factor_copy(0, q).start()
    for way in range(2):
        ring_copy(way, 0, 0).start()
    factor_copy(1, q).start()

    def start_across(p, carry):
        cross_own(p).start()
        return carry

    lax.fori_loop(EARLY_PARTS, parts, start_across, 0)

    def take_factors():
        factor_copy(0, across).wait_recv()
        for way in range(2):
            ring_copy(way, 1, 0).start()
        factor_copy(2, across).start()

    pair_rows[...] = wp_ref[...].astype(jnp.float32)
    spread[...] = jnp.zeros_like(spread)
    for c in range(factor):
        rows = pair_rows[c * factor : (c + 1) * factor, :].astype(jnp.bfloat16)
        for k in range(pack):
            start = (c * pack + k) * factor
            spread[start : start + factor, k * channels : (k + 1) * channels] = rows

    def take_across(p):
        cross(across, p, part_at(p)).wait_recv()
        relay(across, p, part_at(p)).start()

    def make_left():
        for i in range(own_rows):
            rows = gathered[:, q * own_rows + i].reshape(depth, width)
            value = mm_nt(wf_ref[:factor], rows)
            for k in range(depth // 128):
                left_rows[k, pl.ds(i, factor, own_rows), :] = value[:, k * 128 : (k + 1) * 128]
        for k in range(depth // 128):
            left_all[:, k * 128 : (k + 1) * 128] = left_rows[k].astype(jnp.bfloat16)

    jgroups = residues // pack

    def block_at(k):
        last = 2 * hops - 1
        hop = (k - 1) // 2 + 1
        even = jnp.where(lax.rem(k, 2) == 1, blocks - hop, hop)
        shift = jnp.where(k == 0, 0, jnp.where(k == last, hops, even))
        return block_of(lax.rem(place + shift, blocks))

    def pair_wait(k):
        last = 2 * hops - 1

        @pl.when(k == 0)
        def _():
            factor_copy(1, twin).wait_recv()
            factor_copy(2, twin_across).wait_recv()

        for way in range(2):

            @pl.when((k > 0) & (k < last) & (lax.rem(k + 1, 2) == way))
            def _():
                for piece in range(2):
                    share_copy(way, piece, (k - 1) // 2, False).wait_recv()

            @pl.when(k == last)
            def _():
                share_copy(way, way, hops - 1, False).wait_recv()

    def pair_first(k):
        block = block_at(k)
        value = mm(left_all[...], right_all[block].reshape(depth, residues * factor))
        base = pl.multiple_of(lax.rem(k, 2) * (jgroups * own_rows), jgroups * own_rows)
        for c in range(factor):
            for m in range(jgroups // 2):
                outer[
                    pl.ds(base + m * 2 * own_rows, 2 * own_rows), c * 128 : (c + 1) * 128
                ] = jnp.concatenate(
                    [
                        value[c * own_rows : (c + 1) * own_rows, g * 128 : (g + 1) * 128]
                        for g in (2 * m, 2 * m + 1)
                    ],
                    axis=0,
                ).astype(jnp.bfloat16)

    def pair_second(k):
        value = mm(outer[...], spread[...]) * scaling
        for t in range(2):
            for g in range(jgroups):
                start = (t * jgroups + g) * own_rows
                for j in range(pack):
                    products[t, pl.ds(g * pack + j, own_rows, pitch), :] = value[
                        start : start + own_rows, j * channels : (j + 1) * channels
                    ]
        for t in range(2):
            start = pl.multiple_of(block_at(k - 1 + t) * residues, residues)
            for i in range(own_rows):
                pair_ref[i, pl.ds(start, residues), :] = products[
                    t, pl.ds(i * pitch, residues), :
                ].astype(jnp.bfloat16)

    def pair_step(k):
        pair_wait(k)
        pair_first(k)

        @pl.when(lax.rem(k, 2) == 1)
        def _():
            pair_second(k)

    slots = (stages[: len(stages) // 2], stages[len(stages) // 2 :])
    chunks = HEADS * seqs // WIDE

    def residue_at(p, n):
        return part_at(lax.rem(p + parts + n // COUNT, parts)) * COUNT + n % COUNT

    def weigh_last(slot):
        weigh(slot[1], slot[4], chunks - 1, WIDE, seqs, slot[5][...], slot[6][0:1, :])

    def emit(slot, residue):
        update = finish_residue(slot[4], slot[3], wout_ref)
        for piece in range(width // 128):
            strided[piece, pl.ds(residue, seqs, pitch), :] = update[
                :, piece * 128 : (piece + 1) * 128
            ]

    def attend(slot, other, fresh, emitted):
        everything = gathered[:, fresh].reshape(depth, width) if fresh is not None else None
        held = [score(slot[0], slot[2], 0, WIDE)]
        weigh_last(other)
        for c in range(1, chunks):
            now = score(slot[0], slot[2], c, WIDE)
            if c == chunks - 1:
                slot[5][...], slot[6][0:1, :] = now
            if c == 1:
                emit(other, emitted)
                if fresh is not None:
                    prepare_queries(gathered[q, fresh], wq_ref, wg_ref, other[2], other[3])
            held.append(now)
            weigh(slot[1], slot[4], c - 1, WIDE, seqs, *held[c - 1])
            if c == 1 and fresh is not None:
                prepare_keys(everything, wkv_ref, other[0])
        if fresh is not None:
            prepare_values(everything, wkv_ref, other[1])

    take_across(0)
    events = 2 * hops
    loop_events = min((parts - FIRST_EVENT + 1) // 2, events)
    pair_start = half_parts
    loop_pairs = 1
    while (
        pair_start + loop_pairs < parts
        and FIRST_EVENT + 2 * ((loop_pairs - 1) // 2 * 2 + 1) <= pair_start + loop_pairs
    ):
        loop_pairs += 1

    def one_part(p, carry):
        part = part_at(p)

        @pl.when(p + 1 < parts)
        def _():
            take_across(p + 1)

        @pl.when(p == FIRST_EVENT - 1)
        def _():
            take_factors()

        number = p - FIRST_EVENT

        @pl.when((number >= 0) & (lax.rem(number, 2) == 0) & (number // 2 < loop_events))
        def _():
            event(lax.rem(number // 2, 2), number // 4)

        direct(twin, p, part).wait_recv()
        relay(twin_across, p, part).wait_recv()
        for n in range(COUNT):
            attend(slots[(n + 1) % 2], slots[n % 2], residue_at(p, n), residue_at(p, n - 2))

        @pl.when(p == pair_start - 1)
        def _():
            make_left()

        @pl.when((p >= pair_start) & (p - pair_start < loop_pairs))
        def _():
            pair_step(p - pair_start)

        return carry

    lax.fori_loop(0, parts, one_part, 0)

    def late(e, carry):
        event(lax.rem(e, 2), e // 2)
        return carry

    lax.fori_loop(loop_events, events, late, 0)
    attend(slots[1], slots[0], None, residue_at(parts - 1, COUNT - 2))
    weigh_last(slots[1])
    emit(slots[1], residue_at(parts - 1, COUNT - 1))

    def rest(k, carry):
        pair_step(k)
        return carry

    lax.fori_loop(loop_pairs, blocks, rest, 0)

    def finish(i, carry):
        for piece in range(width // 128):
            for k in range(step):
                o_ref[i * step + k, :, piece * 128 : (piece + 1) * 128] = strided[
                    piece, pl.ds((i * step + k) * pitch, residues), :
                ].astype(jnp.bfloat16)
        return carry

    lax.fori_loop(0, seqs // step, finish, 0)

    def drain(p, carry):
        cross_own(p).wait_send()
        direct(q, p, part_at(p)).wait_send()
        relay(across, p, part_at(p)).wait_send()
        return carry

    lax.fori_loop(0, parts, drain, 0)
    for kind, owner in ((0, q), (1, q), (2, across)):
        factor_copy(kind, owner).wait_send()
    for way in range(2):
        for piece in range(2):

            def drain_ring(hop, carry):
                ring_copy(way, piece, hop).wait_send()
                share_copy(way, piece, hop).wait_send()
                return carry

            lax.fori_loop(0, hops if way == piece else hops - 1, drain_ring, 0)


def per_device(alignment, query_weight, w_keyval, w_gate, output_weight, w_factors, w_pair_out):
    seqs, residues, width = alignment.shape
    groups = lax.axis_size("seq")
    blocks = lax.axis_size("res")
    depth = seqs * groups
    factor = w_factors.shape[1] // 2
    hidden = HEADS * HC
    stage = [
        pltpu.VMEM((depth, hidden), jnp.bfloat16),
        pltpu.VMEM((hidden, depth), jnp.bfloat16),
        pltpu.VMEM((HEADS * seqs, hidden), jnp.bfloat16),
        pltpu.VMEM((seqs, hidden), jnp.float32),
        pltpu.VMEM((hidden, 128), jnp.float32),
        pltpu.VMEM((depth, WIDE), jnp.bfloat16),
        pltpu.VMEM((8, WIDE), jnp.float32),
    ]
    channels = w_pair_out.shape[1]
    own_rows = residues // groups
    parts = residues // COUNT
    hops = blocks // 2
    pack = 128 // factor
    pitch = residues + PITCH_PAD
    vmem = pl.BlockSpec(memory_space=pltpu.VMEM)
    dma = pltpu.SemaphoreType.DMA
    return pl.pallas_call(
        functools.partial(block_kernel, 1.0 / depth, blocks, groups),
        in_specs=[vmem] * 7,
        out_specs=[vmem] * 2,
        out_shape=[
            jax.ShapeDtypeStruct((seqs, residues, width), jnp.bfloat16),
            jax.ShapeDtypeStruct((own_rows, blocks * residues, channels), jnp.bfloat16),
        ],
        scratch_shapes=[
            pltpu.VMEM((groups, residues, seqs, width), jnp.bfloat16),
            pltpu.VMEM((width // 128, seqs * pitch, 128), jnp.float32),
            pltpu.VMEM((factor * factor, channels), jnp.float32),
            pltpu.VMEM((factor * 128, pack * channels), jnp.bfloat16),
            pltpu.VMEM((width, pack * 128), jnp.bfloat16),
            pltpu.VMEM((depth // 128, factor * own_rows, 128), jnp.float32),
            pltpu.VMEM((factor * own_rows, depth), jnp.bfloat16),
            pltpu.VMEM((blocks, groups, seqs, residues * factor), jnp.bfloat16),
            pltpu.VMEM((2 * residues // pack * own_rows, factor * 128), jnp.bfloat16),
            pltpu.VMEM((2, own_rows * pitch, channels), jnp.float32),
            dma((parts,)),
            dma((parts,)),
            dma((parts,)),
            dma((parts,)),
            dma((parts,)),
            dma((parts,)),
            dma((3,)),
            dma((3,)),
            dma((2, 2, hops)),
            dma((2, 2, hops)),
            dma((2, 2, hops)),
            dma((2, 2, hops)),
        ]
        + stage * 2,
        compiler_params=pltpu.CompilerParams(
            vmem_limit_bytes=62 * 1024 * 1024, collective_id=0, has_side_effects=True
        ),
        name="block",
    )(alignment, query_weight, w_keyval, w_gate, output_weight, w_factors.T, w_pair_out)


def solution(mesh):
    in_specs = (P("seq", "res", None), P(), P(), P(), P(), P(), P())
    out_specs = (P("seq", "res", None), P(("res", "seq"), None, None))
    return jax.shard_map(
        per_device, mesh=mesh, in_specs=in_specs, out_specs=out_specs, check_vma=False
    )
```

time: 85.3 us -> 62.6 us (0.73)
  Pallas kernels: 81 us -> 58.2 us
    pallas_call x1, Pallas kernels: 81 us -> 58.2 us  [per_device(): pl.pallas_call(functools.partial(block_kernel, 1.0 / depth, blocks, group...]
where the time goes in v2:
time: 62.6 us; the launch traced here: 62.4 us
  Pallas kernels  58.2 us (93%)
  local copies, waits for them, and re-layouts  3.52 us (6%)
  between operations  0.65 us (1%)
    pallas_call x1, Pallas kernels, per_device(): pl.pallas_call(functools.partial(block_kernel, 1.0 / depth, blocks, group...  58.2 us
    unnamed x4, local copies, waits for them, and re-layouts  3.52 us

profile of v2, /device:TPU:0, one launch (start us, length us, event | category | flops | bytes accessed | tf_op | source)
XLA Modules:
  0.0 62.4 jit_solution(13216322851588123839)
XLA Ops:
  0.6 58.2 %block.1 = (bf16[96,32,256]{2,1,0:T(8,128)(2,1)}, bf16[8,256,128]{2,1,0:T(8,128)(2,1)}) custom-call(bf16[96,32,256]{2,1,0:T(8,128)(2,1)} %x_ref.1, bf16[256,256]{1,0:T(8,128)(2,1)} %wq_ref.1, bf16[256,512]{1,0:T(8,128)(2,1)} %wkv_ref.1, bf16[256,256]{1,0:T(8,128)(2,1)} %wg_ref.1, bf16[256,256]{1,0:T(8,128)(2,1)} %wout_ref.1, bf16[64,256]{1,0:T(8,128)(2,1)} %bitcast.1, ...), custom_call_target="tpu_custom_call" | custom-call | tf_op jit(solution)/shard_map/block/pallas_call | solution.py:550
  58.9 0.0 copy-start
  58.9 2.7 %copy.11 = bf16[96,32,256]{2,1,0:T(8,128)(2,1)} copy(bf16[96,32,256]{2,1,0:T(8,128)(2,1)} %get-tuple-element.4) | data formatting | bytes 3145728
  61.6 0.0 copy-done
  61.6 0.8 %copy.12 = bf16[8,256,128]{2,1,0:T(8,128)(2,1)} copy(bf16[8,256,128]{2,1,0:T(8,128)(2,1)S(1)} %copy-done) | data formatting | bytes 1048576
Async XLA Ops:
  58.9 2.7 %copy-start = (bf16[8,256,128]{2,1,0:T(8,128)(2,1)S(1)}, bf16[8,256,128]{2,1,0:T(8,128)(2,1)}, u32[]{:S(2)}) copy-start(bf16[8,256,128]{2,1,0:T(8,128)(2,1)} %get-tuple-element.5) | copy-start | bytes 1572868

commit v3 on v2

--- a/solution.py
+++ b/solution.py
@@ -29,6 +29,7 @@
 PITCH_PAD = 4
 FIRST_EVENT = 3
 EARLY_PARTS = 2
+PIECES = 8
 
 
 SCALE = LOG2E / math.sqrt(HC)
@@ -523,6 +524,19 @@
             lax.fori_loop(0, hops if way == piece else hops - 1, drain_ring, 0)
 
 
+def export_kernel(update, pair, update_out, pair_out, sems):
+    copies = []
+    for k, (source, target) in enumerate(((update, update_out), (pair, pair_out))):
+        rows = source.shape[0] // PIECES
+        for n in range(PIECES):
+            block = pl.ds(n * rows, rows)
+            copies.append(pltpu.make_async_copy(source.at[block], target.at[block], sems.at[k, n]))
+    for copy in copies:
+        copy.start()
+    for copy in copies:
+        copy.wait()
+
+
 def per_device(alignment, query_weight, w_keyval, w_gate, output_weight, w_factors, w_pair_out):
     seqs, residues, width = alignment.shape
     groups = lax.axis_size("seq")
@@ -547,13 +561,13 @@
     pitch = residues + PITCH_PAD
     vmem = pl.BlockSpec(memory_space=pltpu.VMEM)
     dma = pltpu.SemaphoreType.DMA
-    return pl.pallas_call(
+    update, pair = pl.pallas_call(
         functools.partial(block_kernel, 1.0 / depth, blocks, groups),
         in_specs=[vmem] * 7,
         out_specs=[vmem] * 2,
         out_shape=[
-            jax.ShapeDtypeStruct((seqs, residues, width), jnp.bfloat16),
-            jax.ShapeDtypeStruct((own_rows, blocks * residues, channels), jnp.bfloat16),
+            pltpu.VMEM((seqs, residues, width), jnp.bfloat16),
+            pltpu.VMEM((own_rows, blocks * residues, channels), jnp.bfloat16),
         ],
         scratch_shapes=[
             pltpu.VMEM((groups, residues, seqs, width), jnp.bfloat16),
@@ -581,10 +595,26 @@
         ]
         + stage * 2,
         compiler_params=pltpu.CompilerParams(
-            vmem_limit_bytes=62 * 1024 * 1024, collective_id=0, has_side_effects=True
+            vmem_limit_bytes=52 * 1024 * 1024, collective_id=0, has_side_effects=True
         ),
         name="block",
     )(alignment, query_weight, w_keyval, w_gate, output_weight, w_factors.T, w_pair_out)
+    anywhere = pl.BlockSpec(memory_space=pl.ANY)
+    return pl.pallas_call(
+        export_kernel,
+        in_specs=[vmem] * 2,
+        out_specs=[anywhere] * 2,
+        out_shape=[
+            jax.ShapeDtypeStruct(update.shape, update.dtype),
+            jax.ShapeDtypeStruct(pair.shape, pair.dtype),
+        ],
+        scratch_shapes=[dma((2, PIECES))],
+        compiler_params=pltpu.CompilerParams(vmem_limit_bytes=1024 * 1024),
+        name="export",
+    )(
+        pltpu.with_memory_space_constraint(update, pltpu.MemorySpace.VMEM),
+        pltpu.with_memory_space_constraint(pair, pltpu.MemorySpace.VMEM),
+    )
 
 
 def solution(mesh):

time: 62.6 us -> 59.1 us (0.944)
  local copies, waits for them, and re-layouts: 3.52 us -> 0 us
    unnamed x4 -> x0, local copies, waits for them, and re-layouts: 3.52 us -> none
    pallas_call x0 -> x1, Pallas kernels: none -> 1.44 us  [per_device(): pl.pallas_call(export_kernel, in_specs=[vmem] * 2, out_specs=[anywhere] *...]
    pallas_call x1, Pallas kernels: 58.2 us -> 56.9 us  [per_device(): pl.pallas_call(functools.partial(block_kernel, 1.0 / depth, blocks, group...]
where the time goes in v3:
time: 59.1 us; the launch traced here: 59 us
  Pallas kernels  58.3 us (99%)
  between operations  0.64 us (1%)
    pallas_call x1, Pallas kernels, per_device(): pl.pallas_call(functools.partial(block_kernel, 1.0 / depth, blocks, group...  56.9 us
    pallas_call x1, Pallas kernels, per_device(): pl.pallas_call(export_kernel, in_specs=[vmem] * 2, out_specs=[anywhere] *...  1.44 us

profile of v3, /device:TPU:0, one launch (start us, length us, event | category | flops | bytes accessed | tf_op | source)
XLA Modules:
  0.0 59.0 jit_solution(12567727283589485927)
XLA Ops:
  0.6 56.9 %block.1 = (bf16[96,32,256]{2,1,0:T(8,128)(2,1)S(1)}, bf16[8,256,128]{2,1,0:T(8,128)(2,1)S(1)}) custom-call(bf16[96,32,256]{2,1,0:T(8,128)(2,1)} %x_ref.1, bf16[256,256]{1,0:T(8,128)(2,1)} %wq_ref.1, bf16[256,512]{1,0:T(8,128)(2,1)} %wkv_ref.1, bf16[256,256]{1,0:T(8,128)(2,1)} %wg_ref.1, bf16[256,256]{1,0:T(8,128)(2,1)} %wout_ref.1, ...), custom_call_target="tpu_custom_call" | custom-call | tf_op jit(solution)/shard_map/block/pallas_call | solution.py:564
  57.5 1.4 %export.1 = (bf16[96,32,256]{2,1,0:T(8,128)(2,1)}, bf16[8,256,128]{2,1,0:T(8,128)(2,1)}) custom-call(bf16[96,32,256]{2,1,0:T(8,128)(2,1)S(1)} %get-tuple-element.4.update, bf16[8,256,128]{2,1,0:T(8,128)(2,1)S(1)} %get-tuple-element.5.pair), custom_call_target="tpu_custom_call" | custom-call | tf_op jit(solution)/shard_map/export/pallas_call | solution.py:603
